TPU v7x, 512 devices: a whole 4x4x16 slice. The times are simulated.
512 devices in a mesh: dp: 2 (over y_lo), ctx: 16 (over y_hi, x, core), tensor: 16 (over z).
Axes of the slice: x: 4, y: 4 (y_hi: 2, y_lo: 2; y = y_hi * 2 + y_lo), z: 16, core: 2. Of those that a mesh axis runs over, the one named last changes fastest.
Arguments:
- residual: bfloat16 [8192, 3584], P(('dp', 'ctx', 'tensor')), parts along dimension 0, may hold values from -6 to 6
- queries: bfloat16 [8192, 4096], P(('dp', 'ctx'), 'tensor'), parts along dimension 0, may hold values from -8 to 8
- key_heads: bfloat16 [8192, 2048], P(('dp', 'ctx'), 'tensor'), parts along dimension 0, may hold values from -8 to 8
- value_heads: bfloat16 [8192, 2048], P(('dp', 'ctx'), 'tensor'), parts along dimension 0, may hold values from -6 to 6
- doc_blocks: int32 [12], P('dp'), parts along dimension 0, may hold values from 1 to 64, 128 in all
- out_weight: bfloat16 [4096, 3584], P('tensor'), may hold values from -0.265625 to 0.265625
- post_gain: float32 [3584], replicated, may hold values from 0.1 to 1.9
- ffn_gain: float32 [3584], replicated, may hold values from 0.1 to 1.9
- gate_weight: bfloat16 [3584, 14336], P('ctx', 'tensor'), may hold values from -0.09375 to 0.09375
- up_weight: bfloat16 [3584, 14336], P('ctx', 'tensor'), may hold values from -0.09375 to 0.09375
Outputs:
- mixed_stream: bfloat16 [8192, 3584], P(('dp', 'ctx', 'tensor')), parts along dimension 0
- ffn_hidden: bfloat16 [8192, 14336], P(('dp', 'ctx'), 'tensor'), parts along dimension 0
There are 2 independent parts, one for each index of `dp`. A program takes and returns all parts, laid end to end along the dimension named above; an argument that names none is the same for every part. Nothing has to cross between parts.
Inputs may be any that keep to these rules, and one draw needn't show every extreme that they name: `doc_blocks`: the lengths, in blocks of 32 positions, of the 6 documents packed in order into the sequence; they sum to 128, and the longest has exactly 64 blocks.
All inputs are finite; a program needn't handle non-finite values.
Results may differ from a plain program's by a relative error of at most 0.025.
Values may be sent and summed in bfloat16 or wider, within the bound.
No kernel may reach another device: no remote copies, remote signals or barrier semaphores. Data moves between devices by JAX's collectives and lax.ppermute only.
A program may use at most 64 MiB of HBM per device.

v0:
```python
import jax
import jax.numpy as jnp
from jax import lax
from jax.experimental import pallas as pl
from jax.experimental.pallas import tpu as pltpu
from jax.sharding import PartitionSpec as P

BLOCK = 32
SOFT_CAP = 50.0
NORM_EPS = 1e-06
ROPE_BASE = 10000.0
FAR = 4
PIECE = 8


def swap(value, chain):
    n = lax.axis_size("tensor")
    ends = [(i, (i + 1) % n) for i in range(n) if i % 2 == chain]
    return lax.ppermute(value, "tensor", ends + [(j, i) for i, j in ends])


def rope_angles(positions, head_size):
    halfway = head_size // 2
    frequency = ROPE_BASE ** (-(jnp.arange(halfway, dtype=jnp.float32) * 2.0) / head_size)
    angles = positions.astype(jnp.float32)[:, None] * frequency[None, :]
    return (jnp.cos(angles), jnp.sin(angles))


def rotate(first, second, cosine, sine):
    first, second = (first.astype(jnp.float32), second.astype(jnp.float32))
    return jnp.concatenate(
        [first * cosine - second * sine, second * cosine + first * sine], axis=1
    ).astype(jnp.bfloat16)


def doc_of(positions, doc_blocks):
    doc_ends = jnp.cumsum(doc_blocks)
    passed = positions[:, None] // BLOCK >= doc_ends[None, :]
    return jnp.sum(passed.astype(jnp.int32), axis=1)


def rms_scale(values):
    return values * lax.rsqrt(jnp.mean(values * values, axis=-1, keepdims=True) + NORM_EPS)


def gated(total, ff):
    gate, up = (total[:, :ff], total[:, ff:])
    inner = 0.7978845608028654 * (gate + 0.044715 * gate * gate * gate)
    return (0.5 * gate * (1.0 + jnp.tanh(inner)) * up).astype(jnp.bfloat16)


def ffn_kernel(steps, ff, joined, parity_ref, *refs):
    pieces, (weight_ref, *rest) = (refs[:joined], refs[joined:])
    done_ref, out_ref, total = rest if len(rest) == 3 else (None, *rest)
    k = pl.program_id(0)
    a = jnp.concatenate([p[...] for p in pieces], axis=0) if joined > 1 else pieces[0][...]
    product = jnp.dot(a, weight_ref[...], preferred_element_type=jnp.float32)

    @pl.when(k == 0)
    def _():
        total[...] = product

    @pl.when(k > 0)
    def _():
        total[...] += product

    @pl.when(k == steps - 1)
    def _():
        hidden = gated(total[...], ff)
        if done_ref is None:
            out_ref[...] = hidden
        else:
            parity = parity_ref[0]
            out_ref[:, parity] = done_ref[...].reshape(8, 16, ff)
            out_ref[:, 1 - parity] = hidden.reshape(8, 16, ff)


def ffn(parity, pieces, weights, done):
    depth, width = weights.shape
    ff = width // 2
    rows = sum(p.shape[0] for p in pieces)
    step = 512
    steps = depth // step
    whole = [] if done is None else [done]
    shape = (rows, ff) if done is None else (8, 2, 16, ff)
    return pl.pallas_call(
        lambda *refs: ffn_kernel(steps, ff, len(pieces), *refs),
        out_shape=jax.ShapeDtypeStruct(shape, jnp.bfloat16),
        grid=(steps,),
        in_specs=[pl.BlockSpec(memory_space=pltpu.SMEM)]
        + [pl.BlockSpec((p.shape[0], step), lambda k: (0, k)) for p in pieces]
        + [pl.BlockSpec((step, width), lambda k: (k, 0))]
        + [pl.BlockSpec((rows, ff), lambda k: (0, 0)) for _ in whole],
        out_specs=pl.BlockSpec(shape, lambda k: (0,) * len(shape)),
        scratch_shapes=[pltpu.VMEM((rows, width), jnp.float32)],
        cost_estimate=pl.CostEstimate(
            flops=2 * rows * depth * width,
            bytes_accessed=2 * depth * width,
            transcendentals=rows * ff,
        ),
        name="ffn",
    )(parity, *pieces, weights, *whole)


def per_device(
    residual,
    queries,
    key_heads,
    value_heads,
    doc_blocks,
    out_weight,
    post_gain,
    ffn_gain,
    gate_weight,
    up_weight,
):
    f32 = jnp.float32
    bf16 = jnp.bfloat16
    rows = queries.shape[0]
    hd = queries.shape[1]
    d = residual.shape[1]
    ff = gate_weight.shape[1]
    half = hd // 2
    c = lax.axis_index("ctx")
    t = lax.axis_index("tensor")
    n_ctx = lax.axis_size("ctx")
    stride4 = [[j + 4 * q for q in range(4)] for j in range(4)]

    partner = swap(jnp.stack([key_heads, value_heads]), 0)
    partner, gate_weight, up_weight = lax.optimization_barrier((partner, gate_weight, up_weight))
    weights = lax.all_gather(
        jnp.concatenate([gate_weight, up_weight], axis=1), "ctx", axis=0, tiled=True
    )
    own_first = t % 2 == 0
    pos = c * rows + jnp.arange(rows, dtype=jnp.int32)
    cosine, sine = rope_angles(pos, hd)
    k_lo = jnp.where(own_first, key_heads, partner[0])
    k_hi = jnp.where(own_first, partner[0], key_heads)
    v_lo = jnp.where(own_first, value_heads, partner[1])
    v_hi = jnp.where(own_first, partner[1], value_heads)
    block = jnp.concatenate([rotate(k_lo, k_hi, cosine, sine), v_lo, v_hi], axis=1)
    came = [
        lax.ppermute(block, "ctx", [(i, i + 2 * s) for i in range(n_ctx - 2 * s)])
        for s in range(FAR, 0, -1)
    ] + [block]
    mine = jnp.concatenate(came, axis=0)
    other = lax.ppermute(mine, "ctx", [(i, i ^ 1) for i in range(n_ctx)])
    chip = c // 2
    core = c % 2
    first_of = (chip - FAR + jnp.arange(FAR + 1, dtype=jnp.int32)) * 2
    inner = jnp.arange(rows, dtype=jnp.int32)
    pos_mine = ((first_of + core) * rows)[:, None] + inner[None, :]
    pos_other = ((first_of + 1 - core) * rows)[:, None] + inner[None, :]
    key_pos = jnp.concatenate([pos_mine.reshape(-1), pos_other.reshape(-1)])
    kv = jnp.concatenate([mine, other], axis=0)
    key_rows, value_rows = (kv[:, :hd], kv[:, hd:])

    way = [1 - 2 * ((t + chain) % 2) for chain in range(2)]

    def leave(a):
        a = a.reshape(4, 4, 2, PIECE, *a.shape[1:])

        def of(chain, r):
            one = lax.dynamic_index_in_dim(a[:, :, chain], (t + r) % 4, 1, keepdims=False)
            return one.reshape(4 * PIECE, *a.shape[4:])

        return jnp.concatenate(
            [of(x, r) for x in range(2) for r in (2, 4 + way[x])]
            + [of(x, r) for x in range(2) for r in (4 - way[x], 0)],
            axis=0,
        )

    q_rows = leave(rotate(queries[:, :half], queries[:, half:], cosine, sine))
    q_pos = leave(pos)
    q_doc = doc_of(q_pos, doc_blocks)
    key_doc = doc_of(jnp.maximum(key_pos, 0), doc_blocks)
    scores = lax.dot_general(
        q_rows, key_rows, (((1,), (1,)), ((), ())), preferred_element_type=f32
    ) * (hd ** (-0.5))
    capped = SOFT_CAP * jnp.tanh(scores / SOFT_CAP)
    visible = (
        (key_pos[None, :] <= q_pos[:, None])
        & (key_doc[None, :] == q_doc[:, None])
        & (key_pos[None, :] >= 0)
    )
    probs = jnp.where(visible, jnp.exp(capped), 0.0).astype(bf16)
    numerator = jnp.dot(probs, value_rows, preferred_element_type=f32)
    denominator = jnp.sum(probs.astype(f32), axis=1)
    attended = (numerator / denominator[:, None]).astype(bf16)

    def out(a):
        return jnp.dot(attended[a : a + 64], out_weight, preferred_element_type=f32).astype(bf16)

    sent = [swap(out(64 * x), x) for x in range(2)]
    kept = [out(128 + 64 * x) for x in range(2)]
    both = [kept[x].astype(f32) + sent[x].astype(f32) for x in range(2)]
    again = [swap(both[x][:32].astype(bf16), 1 - x) for x in range(2)]
    sums = [(both[x][32:] + again[x].astype(f32)).astype(bf16) for x in range(2)]

    sums = jnp.stack([a.reshape(4, PIECE, d) for a in sums], axis=1).reshape(4, 2 * PIECE, d)
    parts = lax.all_to_all(sums, "tensor", 0, 0, tiled=True, axis_index_groups=stride4)
    attn_rows = jnp.sum(parts.astype(f32), axis=0)
    mixed = (residual.astype(f32) + rms_scale(attn_rows) * post_gain).astype(bf16)
    ffn_in = (rms_scale(mixed.astype(f32)) * ffn_gain).astype(bf16)

    stride2 = [[j + 2 * m for m in range(8)] for j in range(2)]
    own = lax.all_gather(ffn_in, "tensor", axis=0, tiled=True, axis_index_groups=stride2)
    own, weights = lax.optimization_barrier((own, weights))
    rest = [swap(own[64 * x : 64 * (x + 1)], x) for x in range(2)]
    parity = (t % 2).astype(jnp.int32).reshape(1)
    done = ffn(parity, [own], weights, None)
    hidden = ffn(parity, rest, weights, done)
    return (mixed, hidden.reshape(rows, ff))


def solution(mesh):
    in_specs = (
        P(("dp", "ctx", "tensor"), None),
        P(("dp", "ctx"), "tensor"),
        P(("dp", "ctx"), "tensor"),
        P(("dp", "ctx"), "tensor"),
        P("dp"),
        P("tensor", None),
        P(),
        P(),
        P("ctx", "tensor"),
        P("ctx", "tensor"),
    )
    out_specs = (P(("dp", "ctx", "tensor"), None), P(("dp", "ctx"), "tensor"))
    return jax.shard_map(
        per_device, mesh=mesh, in_specs=in_specs, out_specs=out_specs, check_vma=False
    )
```

profile of v0, /device:TPU:24, one launch (start us, length us, event | category | flops | bytes accessed | tf_op | source)
XLA Modules:
  0.0 196.6 jit_solution(18056923186009521814)
XLA Ops:
  7.2 0.0 copy-start
  7.2 0.0 all-gather.2.cloned.1.call-start
  7.3 1.0 pad_maximum_fusion.2
  8.3 0.0 copy-start.9
  8.3 3.8 %collective-permute-start = (bf16[2,256,128]{2,1,0:T(8,128)(2,1)S(1)}, bf16[2,256,128]{2,1,0:T(8,128)(2,1)S(1)}, u32[]{:S(2)}, u32[]{:S(2)}) collective-permute-start(bf16[2,256,128]{2,1,0:T(8,128)(2,1)S(1)} %pad_maximum_fusion.2), channel_id=1, source_target_pairs={{0,1},{2,3},{4,5},{6,7},{8,9},{10,11},{12,13},{14,15},{1,0},{3,2},... | collective-permute-start | bytes 393224 | tf_op jit(solution)/shard_map/ppermute | solution.py:19
  12.1 3.5 %collective-permute-done = bf16[2,256,128]{2,1,0:T(8,128)(2,1)S(1)} collective-permute-done((bf16[2,256,128]{2,1,0:T(8,128)(2,1)S(1)}, bf16[2,256,128]{2,1,0:T(8,128)(2,1)S(1)}, u32[]{:S(2)}, u32[]{:S(2)}) %collective-permute-start) | collective-permute-done | bytes 131104 | tf_op jit(solution)/shard_map/ppermute | solution.py:19
  15.6 2.1 %pad_maximum_fusion = bf16[224,1792]{1,0:T(8,128)(2,1)} fusion(bf16[224,896]{1,0:T(8,128)(2,1)} %param.19, bf16[224,896]{1,0:T(8,128)(2,1)} %param.18), kind=kLoop, calls=%fused_computation.21 | loop fusion | flops 1605632 | bytes 1605632 | tf_op jit(solution)/shard_map/concatenate | solution.py:132
  17.7 0.0 all-gather.2.cloned.1.call-update
  17.9 0.1 reshape.501
  18.0 0.1 reshape.502
  18.1 0.1 reshape.503
  18.2 0.1 reshape.504
  18.3 0.1 reshape.505
  18.3 0.1 reshape.506
  18.4 0.1 reshape.507
  18.5 0.1 reshape.508
  18.6 0.1 iota_add_fusion.1
  18.7 0.1 iota_add_fusion
  18.7 0.1 concatenate.56
  19.0 0.6 fusion.36
  19.6 1.3 collective-permute-start.1
  20.9 4.7 %collective-permute-start.2 = (bf16[256,512]{1,0:T(8,128)(2,1)S(1)}, bf16[256,512]{1,0:T(8,128)(2,1)S(1)}, u32[]{:S(2)}, u32[]{:S(2)}) collective-permute-start(bf16[256,512]{1,0:T(8,128)(2,1)S(1)} %pad_maximum_fusion.1), channel_id=1, source_target_pairs={{0,96},{16,112},{32,128},{48,144},{64,160},{80,176},{96,192},{112,... | collective-permute-start | bytes 786440 | tf_op jit(solution)/shard_map/ppermute | solution.py:143
  25.6 0.2 reduce-window.8
  25.8 1.9 collective-permute-start.3
  27.7 0.1 convert_reduce_fusion.2
  27.8 2.1 %collective-permute-start.4 = (bf16[256,512]{1,0:T(8,128)(2,1)S(1)}, bf16[256,512]{1,0:T(8,128)(2,1)S(1)}, u32[]{:S(2)}, u32[]{:S(2)}) collective-permute-start(bf16[256,512]{1,0:T(8,128)(2,1)S(1)} %pad_maximum_fusion.1), channel_id=1, source_target_pairs={{0,32},{16,48},{32,64},{48,80},{64,96},{80,112},{96,128},{112,144}... | collective-permute-start | bytes 786440 | tf_op jit(solution)/shard_map/ppermute | solution.py:143
  30.0 21.7 %collective-permute-done.1 = bf16[256,512]{1,0:T(8,128)(2,1)S(1)} collective-permute-done((bf16[256,512]{1,0:T(8,128)(2,1)S(1)}, bf16[256,512]{1,0:T(8,128)(2,1)S(1)}, u32[]{:S(2)}, u32[]{:S(2)}) %collective-permute-start.1) | collective-permute-done | bytes 262176 | tf_op jit(solution)/shard_map/ppermute | solution.py:143
  51.7 0.0 collective-permute-done.2
  51.8 0.0 collective-permute-done.3
  51.8 0.0 collective-permute-done.4
  51.9 1.9 collective-permute-start.5
  53.8 0.1 convert_reduce_fusion.3
  54.1 2.7 %collective-permute-done.5 = bf16[1280,512]{1,0:T(8,128)(2,1)S(1)} collective-permute-done((bf16[1280,512]{1,0:T(8,128)(2,1)S(1)}, bf16[1280,512]{1,0:T(8,128)(2,1)S(1)}, u32[]{:S(2)}, u32[]{:S(2)}) %collective-permute-start.5) | collective-permute-done | bytes 1310752 | tf_op jit(solution)/shard_map/ppermute | solution.py:147
  56.8 0.1 constant_dynamic-update-slice_fusion.14
  56.9 1.5 convert_reduce_fusion
  58.4 0.5 fusion.13
  59.0 0.4 convolution_convert_fusion.2
  59.4 3.6 %collective-permute-start.6 = (bf16[64,3584]{1,0:T(8,128)(2,1)S(1)}, bf16[64,3584]{1,0:T(8,128)(2,1)S(1)}, u32[]{:S(2)}, u32[]{:S(2)}) collective-permute-start(bf16[64,3584]{1,0:T(8,128)(2,1)S(1)} %convolution_convert_fusion.2), channel_id=1, source_target_pairs={{0,1},{2,3},{4,5},{6,7},{8,9},{10,11},{12,13},{14,15},{1,0},{3,2},... | collective-permute-start | bytes 1376264 | tf_op jit(solution)/shard_map/ppermute | solution.py:19
  63.1 0.4 convolution_convert_fusion
  63.5 10.5 %collective-permute-start.8 = (bf16[64,3584]{1,0:T(8,128)(2,1)S(1)}, bf16[64,3584]{1,0:T(8,128)(2,1)S(1)}, u32[]{:S(2)}, u32[]{:S(2)}) collective-permute-start(bf16[64,3584]{1,0:T(8,128)(2,1)S(1)} %convolution_convert_fusion), channel_id=1, source_target_pairs={{1,2},{3,4},{5,6},{7,8},{9,10},{11,12},{13,14},{15,0},{2,1},{4,3},... | collective-permute-start | bytes 1376264 | tf_op jit(solution)/shard_map/ppermute | solution.py:19
  74.0 0.0 collective-permute-done.6
  74.0 0.4 convert_add_fusion.1
  74.5 11.1 %collective-permute-start.7 = (bf16[32,3584]{1,0:T(8,128)(2,1)S(1)}, bf16[32,3584]{1,0:T(8,128)(2,1)S(1)}, u32[]{:S(2)}, u32[]{:S(2)}) collective-permute-start(bf16[32,3584]{1,0:T(8,128)(2,1)S(1)} %slice.165), channel_id=1, source_target_pairs={{1,2},{3,4},{5,6},{7,8},{9,10},{11,12},{13,14},{15,0},{2,1},{4,3},... | collective-permute-start | bytes 688136 | tf_op jit(solution)/shard_map/ppermute | solution.py:19
  85.6 0.0 collective-permute-done.8
  85.6 0.4 convert_add_fusion
  86.1 1.9 collective-permute-start.9
  88.0 2.6 %collective-permute-done.7 = bf16[32,3584]{1,0:T(8,128)(2,1)S(1)} collective-permute-done((bf16[32,3584]{1,0:T(8,128)(2,1)S(1)}, bf16[32,3584]{1,0:T(8,128)(2,1)S(1)}, u32[]{:S(2)}, u32[]{:S(2)}) %collective-permute-start.7) | collective-permute-done | bytes 229408 | tf_op jit(solution)/shard_map/ppermute | solution.py:19
  90.7 0.0 copy-start.6
  90.7 0.0 copy-start.8
  90.7 3.8 %collective-permute-done.9 = bf16[32,3584]{1,0:T(8,128)(2,1)S(1)} collective-permute-done((bf16[32,3584]{1,0:T(8,128)(2,1)S(1)}, bf16[32,3584]{1,0:T(8,128)(2,1)S(1)}, u32[]{:S(2)}, u32[]{:S(2)}) %collective-permute-start.9) | collective-permute-done | bytes 229408 | tf_op jit(solution)/shard_map/ppermute | solution.py:19
  94.5 0.1 fusion.22
  94.5 0.0 copy-start.7
  94.6 30.3 %all_to_all.5 = bf16[4,16,3584]{2,1,0:T(8,128)(2,1)S(1)} all-to-all(bf16[4,16,3584]{2,1,0:T(8,128)(2,1)S(1)} %maximum_bitcast_fusion), channel_id=1, replica_groups={{0,4,8,12},{1,5,9,13},{2,6,10,14},{3,7,11,15},{16,20,24,28},{17,21,25,2..., dimensions={0} | all-to-all | bytes 917504 | tf_op jit(solution)/shard_map/all_to_all | solution.py:201
  124.9 0.1 convert_reduce_fusion.1
  125.0 0.1 multiply_reduce_fusion
  125.2 0.2 fusion.18
  125.4 0.1 fusion.20
  125.5 35.7 %all_gather.6.refs_1_ = bf16[128,3584]{1,0:T(8,128)(2,1)S(1)} all-gather(bf16[16,3584]{1,0:T(8,128)(2,1)S(1)} %fusion.20), channel_id=1, replica_groups={{0,2,4,6,8,10,12,14},{1,3,5,7,9,11,13,15},{16,18,20,22,24,26,28,30},{17..., dimensions={0}, use_global_device_ids=true | all-gather | bytes 1032192 | tf_op jit(solution)/shard_map/all_gather | solution.py:207
  161.2 0.9 fusion.57
  162.1 3.6 %collective-permute-start.10 = (bf16[64,3584]{1,0:T(8,128)(2,1)}, bf16[64,3584]{1,0:T(8,128)(2,1)}, u32[]{:S(2)}, u32[]{:S(2)}) collective-permute-start(bf16[64,3584]{1,0:T(8,128)(2,1)} %get-tuple-element.15), channel_id=1, source_target_pairs={{0,1},{2,3},{4,5},{6,7},{8,9},{10,11},{12,13},{14,15},{1,0},{3,2},... | collective-permute-start | bytes 1376264 | tf_op jit(solution)/shard_map/ppermute | solution.py:19
  165.8 5.3 %collective-permute-start.11 = (bf16[64,3584]{1,0:T(8,128)(2,1)S(1)}, bf16[64,3584]{1,0:T(8,128)(2,1)}, u32[]{:S(2)}, u32[]{:S(2)}) collective-permute-start(bf16[64,3584]{1,0:T(8,128)(2,1)S(1)} %get-tuple-element.14), channel_id=1, source_target_pairs={{1,2},{3,4},{5,6},{7,8},{9,10},{11,12},{13,14},{15,0},{2,1},{4,3},... | collective-permute-start | bytes 1376264 | tf_op jit(solution)/shard_map/ppermute | solution.py:19
  171.1 9.2 %ffn.2.refs_4_ = bf16[128,896]{1,0:T(8,128)(2,1)} custom-call(s32[1]{0:T(128)} %bitcast.21.refs_0_, bf16[128,3584]{1,0:T(8,128)(2,1)} %copy-done.1, bf16[3584,1792]{1,0:T(8,128)(2,1)} %all-gather.2.cloned.1.call-done.refs_2_.refs_3_), custom_call_target="tpu_custom_call" | custom-call | flops 1644167168 | bytes 12845056 | tf_op jit(solution)/shard_map/ffn/pallas_call | solution.py:86
  180.3 0.0 collective-permute-done.10.refs_1_
  180.3 9.4 %ffn.3 = bf16[8,2,16,896]{3,2,1,0:T(8,128)(2,1)} custom-call(s32[1]{0:T(128)} %bitcast.21.refs_0_, bf16[64,3584]{1,0:T(8,128)(2,1)} %collective-permute-done.10.refs_1_, bf16[64,3584]{1,0:T(8,128)(2,1)} %collective-permute-done.11.refs_2_, bf16[3584,1792]{1,0:T(8,128)(2,1)} %all-gather.2.cloned.1.call-done.refs_2_.refs_3_, bf16[128,896]{1,0:T(8,128)(2,1)} %ffn.2.refs_4_), custom_call_target="tpu_custom_call" | custom-call | flops 1644167168 | bytes 12845056 | tf_op jit(solution)/shard_map/ffn/pallas_call | solution.py:86
  (53 shorter events, 0.7 us)
Async XLA Ops:
  7.2 51.8 %copy-start = (bf16[256,3584]{1,0:T(8,128)(2,1)S(1)}, bf16[256,3584]{1,0:T(8,128)(2,1)}, u32[]{:S(2)}) copy-start(bf16[256,3584]{1,0:T(8,128)(2,1)} %param.15) | copy-start | bytes 5505028
  7.2 11.8 %copy-start.4 = (bf16[256,128]{1,0:T(8,128)(2,1)S(1)}, bf16[256,128]{1,0:T(8,128)(2,1)}, u32[]{:S(2)}) copy-start(bf16[256,128]{1,0:T(8,128)(2,1)} %param.12) | copy-start | bytes 196612
  7.2 11.7 %copy-start.3 = (bf16[256,128]{1,0:T(8,128)(2,1)S(1)}, bf16[256,128]{1,0:T(8,128)(2,1)}, u32[]{:S(2)}) copy-start(bf16[256,128]{1,0:T(8,128)(2,1)} %param.13) | copy-start | bytes 196612
  7.2 11.8 %copy-start.5 = (bf16[256,256]{1,0:T(8,128)(2,1)S(1)}, bf16[256,256]{1,0:T(8,128)(2,1)}, u32[]{:S(2)}) copy-start(bf16[256,256]{1,0:T(8,128)(2,1)} %param.11) | copy-start | bytes 393220
  7.2 154.0 %all-gather.2.cloned.1.call-start = ((), (), s32[]{:S(2)}) async-start(), calls=%async_computation.1 | async-start | bytes 13647872 | tf_op jit(solution)/shard_map/all_gather | solution.py:131
  8.3 17.4 %copy-start.9 = (s32[6]{0:T(128)S(1)}, s32[6]{0:T(128)}, u32[]{:S(2)}) copy-start(s32[6]{0:T(128)} %param.14) | copy-start | bytes 76
  8.3 7.3 %collective-permute-start = (bf16[2,256,128]{2,1,0:T(8,128)(2,1)S(1)}, bf16[2,256,128]{2,1,0:T(8,128)(2,1)S(1)}, u32[]{:S(2)}, u32[]{:S(2)}) collective-permute-start(bf16[2,256,128]{2,1,0:T(8,128)(2,1)S(1)} %pad_maximum_fusion.2), channel_id=1, source_target_pairs={{0,1},{2,3},{4,5},{6,7},{8,9},{10,11},{12,13},{14,15},{1,0},{3,2},... | collective-permute-start | bytes 393224 | tf_op jit(solution)/shard_map/ppermute | solution.py:19
  19.6 32.0 %collective-permute-start.1 = (bf16[256,512]{1,0:T(8,128)(2,1)S(1)}, bf16[256,512]{1,0:T(8,128)(2,1)S(1)}, u32[]{:S(2)}, u32[]{:S(2)}) collective-permute-start(bf16[256,512]{1,0:T(8,128)(2,1)S(1)} %pad_maximum_fusion.1), channel_id=1, source_target_pairs={{0,128},{16,144},{32,160},{48,176},{64,192},{80,208},{96,224},{112... | collective-permute-start | bytes 786440 | tf_op jit(solution)/shard_map/ppermute | solution.py:143
  20.9 30.8 %collective-permute-start.2 = (bf16[256,512]{1,0:T(8,128)(2,1)S(1)}, bf16[256,512]{1,0:T(8,128)(2,1)S(1)}, u32[]{:S(2)}, u32[]{:S(2)}) collective-permute-start(bf16[256,512]{1,0:T(8,128)(2,1)S(1)} %pad_maximum_fusion.1), channel_id=1, source_target_pairs={{0,96},{16,112},{32,128},{48,144},{64,160},{80,176},{96,192},{112,... | collective-permute-start | bytes 786440 | tf_op jit(solution)/shard_map/ppermute | solution.py:143
  25.8 25.9 %collective-permute-start.3 = (bf16[256,512]{1,0:T(8,128)(2,1)S(1)}, bf16[256,512]{1,0:T(8,128)(2,1)S(1)}, u32[]{:S(2)}, u32[]{:S(2)}) collective-permute-start(bf16[256,512]{1,0:T(8,128)(2,1)S(1)} %pad_maximum_fusion.1), channel_id=1, source_target_pairs={{0,64},{16,80},{32,96},{48,112},{64,128},{80,144},{96,160},{112,17... | collective-permute-start | bytes 786440 | tf_op jit(solution)/shard_map/ppermute | solution.py:143
  27.8 24.0 %collective-permute-start.4 = (bf16[256,512]{1,0:T(8,128)(2,1)S(1)}, bf16[256,512]{1,0:T(8,128)(2,1)S(1)}, u32[]{:S(2)}, u32[]{:S(2)}) collective-permute-start(bf16[256,512]{1,0:T(8,128)(2,1)S(1)} %pad_maximum_fusion.1), channel_id=1, source_target_pairs={{0,32},{16,48},{32,64},{48,80},{64,96},{80,112},{96,128},{112,144}... | collective-permute-start | bytes 786440 | tf_op jit(solution)/shard_map/ppermute | solution.py:143
  51.9 4.9 %collective-permute-start.5 = (bf16[1280,512]{1,0:T(8,128)(2,1)S(1)}, bf16[1280,512]{1,0:T(8,128)(2,1)S(1)}, u32[]{:S(2)}, u32[]{:S(2)}) collective-permute-start(bf16[1280,512]{1,0:T(8,128)(2,1)S(1)} %get-tuple-element.16), channel_id=1, source_target_pairs={{0,16},{16,0},{32,48},{48,32},{64,80},{80,64},{96,112},{112,96},{1... | collective-permute-start | bytes 3932168 | tf_op jit(solution)/shard_map/ppermute | solution.py:147
  59.4 14.6 %collective-permute-start.6 = (bf16[64,3584]{1,0:T(8,128)(2,1)S(1)}, bf16[64,3584]{1,0:T(8,128)(2,1)S(1)}, u32[]{:S(2)}, u32[]{:S(2)}) collective-permute-start(bf16[64,3584]{1,0:T(8,128)(2,1)S(1)} %convolution_convert_fusion.2), channel_id=1, source_target_pairs={{0,1},{2,3},{4,5},{6,7},{8,9},{10,11},{12,13},{14,15},{1,0},{3,2},... | collective-permute-start | bytes 1376264 | tf_op jit(solution)/shard_map/ppermute | solution.py:19
  63.5 22.1 %collective-permute-start.8 = (bf16[64,3584]{1,0:T(8,128)(2,1)S(1)}, bf16[64,3584]{1,0:T(8,128)(2,1)S(1)}, u32[]{:S(2)}, u32[]{:S(2)}) collective-permute-start(bf16[64,3584]{1,0:T(8,128)(2,1)S(1)} %convolution_convert_fusion), channel_id=1, source_target_pairs={{1,2},{3,4},{5,6},{7,8},{9,10},{11,12},{13,14},{15,0},{2,1},{4,3},... | collective-permute-start | bytes 1376264 | tf_op jit(solution)/shard_map/ppermute | solution.py:19
  74.5 16.1 %collective-permute-start.7 = (bf16[32,3584]{1,0:T(8,128)(2,1)S(1)}, bf16[32,3584]{1,0:T(8,128)(2,1)S(1)}, u32[]{:S(2)}, u32[]{:S(2)}) collective-permute-start(bf16[32,3584]{1,0:T(8,128)(2,1)S(1)} %slice.165), channel_id=1, source_target_pairs={{1,2},{3,4},{5,6},{7,8},{9,10},{11,12},{13,14},{15,0},{2,1},{4,3},... | collective-permute-start | bytes 688136 | tf_op jit(solution)/shard_map/ppermute | solution.py:19
  86.1 8.4 %collective-permute-start.9 = (bf16[32,3584]{1,0:T(8,128)(2,1)S(1)}, bf16[32,3584]{1,0:T(8,128)(2,1)S(1)}, u32[]{:S(2)}, u32[]{:S(2)}) collective-permute-start(bf16[32,3584]{1,0:T(8,128)(2,1)S(1)} %slice.164), channel_id=1, source_target_pairs={{0,1},{2,3},{4,5},{6,7},{8,9},{10,11},{12,13},{14,15},{1,0},{3,2},... | collective-permute-start | bytes 688136 | tf_op jit(solution)/shard_map/ppermute | solution.py:19
  90.7 34.5 %copy-start.6 = (bf16[16,3584]{1,0:T(8,128)(2,1)S(1)}, bf16[16,3584]{1,0:T(8,128)(2,1)}, u32[]{:S(2)}) copy-start(bf16[16,3584]{1,0:T(8,128)(2,1)} %param.10) | copy-start | bytes 344068
  90.7 34.5 %copy-start.8 = (f32[3584]{0:T(1024)S(1)}, f32[3584]{0:T(1024)}, u32[]{:S(2)}) copy-start(f32[3584]{0:T(1024)} %param.16) | copy-start | bytes 43012
  94.5 30.9 %copy-start.7 = (f32[3584]{0:T(1024)S(1)}, f32[3584]{0:T(1024)}, u32[]{:S(2)}) copy-start(f32[3584]{0:T(1024)} %param.17) | copy-start | bytes 43012
  125.4 54.9 %copy-start.2 = (bf16[16,3584]{1,0:T(8,128)(2,1)}, bf16[16,3584]{1,0:T(8,128)(2,1)S(1)}, u32[]{:S(2)}) copy-start(bf16[16,3584]{1,0:T(8,128)(2,1)S(1)} %get-tuple-element.13) | copy-start | bytes 344068
  161.2 9.8 %copy-start.1 = (bf16[128,3584]{1,0:T(8,128)(2,1)}, bf16[128,3584]{1,0:T(8,128)(2,1)S(1)}, u32[]{:S(2)}) copy-start(bf16[128,3584]{1,0:T(8,128)(2,1)S(1)} %all_gather.6.refs_1_) | copy-start | bytes 2752516
  162.1 18.2 %collective-permute-start.10 = (bf16[64,3584]{1,0:T(8,128)(2,1)}, bf16[64,3584]{1,0:T(8,128)(2,1)}, u32[]{:S(2)}, u32[]{:S(2)}) collective-permute-start(bf16[64,3584]{1,0:T(8,128)(2,1)} %get-tuple-element.15), channel_id=1, source_target_pairs={{0,1},{2,3},{4,5},{6,7},{8,9},{10,11},{12,13},{14,15},{1,0},{3,2},... | collective-permute-start | bytes 1376264 | tf_op jit(solution)/shard_map/ppermute | solution.py:19
  165.8 14.5 %collective-permute-start.11 = (bf16[64,3584]{1,0:T(8,128)(2,1)S(1)}, bf16[64,3584]{1,0:T(8,128)(2,1)}, u32[]{:S(2)}, u32[]{:S(2)}) collective-permute-start(bf16[64,3584]{1,0:T(8,128)(2,1)S(1)} %get-tuple-element.14), channel_id=1, source_target_pairs={{1,2},{3,4},{5,6},{7,8},{9,10},{11,12},{13,14},{15,0},{2,1},{4,3},... | collective-permute-start | bytes 1376264 | tf_op jit(solution)/shard_map/ppermute | solution.py:19
Sparse Core Ops, SparseCore 0:
  17.8 116.1 all-gather.1
where the time goes:
time: 197 us
  blocking collectives  66 us (34%)
  starting transfers between devices  51.8 us (26%)
  waiting for transfers between devices  34.3 us (17%)
  Pallas kernels  18.6 us (9%)
  between operations  14.7 us (7%)
  other arithmetic  5.13 us (3%)
  matrix products  3.81 us (2%)
  local copies, waits for them, and re-layouts  2.07 us (1%)
    ppermute x7, starting transfers between devices, swap(): return lax.ppermute(value, 'tensor', ends + [(j, i) for i, j in ends])  39.9 us
    all_gather x1, blocking collectives, per_device(): lax.all_gather(ffn_in, 'tensor', axis=0, tiled=True, axis_index_groups=st...  35.7 us
    all_to_all x1, blocking collectives, per_device(): lax.all_to_all(sums, 'tensor', 0, 0, tiled=True, axis_index_groups=stride4)  30.3 us
    ppermute x4, waiting for transfers between devices, per_device(): lax.ppermute(block, 'ctx', [(i, i + 2 * s) for i in range(n_ctx - 2 * s)])  21.7 us
    pallas_call x2, Pallas kernels, ffn(): pl.pallas_call(lambda *refs: ffn_kernel(steps, ff, len(pieces), *refs), o...  18.6 us
    ppermute x4, starting transfers between devices, per_device(): lax.ppermute(block, 'ctx', [(i, i + 2 * s) for i in range(n_ctx - 2 * s)])  10 us
    ppermute x7, waiting for transfers between devices, swap(): return lax.ppermute(value, 'tensor', ends + [(j, i) for i, j in ends])  9.9 us
  transfers between devices with their start and end apart: 13, of which 5 were waited for; matrix products, arithmetic and copies ran while one was open for 4% of the time, Pallas kernels for 5%

commit v1 on v0

--- a/solution.py
+++ b/solution.py
@@ -10,12 +10,21 @@
 NORM_EPS = 1e-06
 ROPE_BASE = 10000.0
 FAR = 4
-PIECE = 8
+
+
+def twin(v):
+    return v ^ (v >> 3)
 
 
 def swap(value, chain):
     n = lax.axis_size("tensor")
     ends = [(i, (i + 1) % n) for i in range(n) if i % 2 == chain]
+    return lax.ppermute(value, "tensor", ends + [(j, i) for i, j in ends])
+
+
+def swap_pairs(value, chain):
+    n = lax.axis_size("tensor")
+    ends = [(twin(v), twin((v + 2) % n)) for v in range(n) if (v // 2) % 2 == chain]
     return lax.ppermute(value, "tensor", ends + [(j, i) for i, j in ends])
 
 
@@ -79,7 +88,7 @@
     depth, width = weights.shape
     ff = width // 2
     rows = sum(p.shape[0] for p in pieces)
-    step = 512
+    step = 896
     steps = depth // step
     whole = [] if done is None else [done]
     shape = (rows, ff) if done is None else (8, 2, 16, ff)
@@ -124,13 +133,22 @@
     c = lax.axis_index("ctx")
     t = lax.axis_index("tensor")
     n_ctx = lax.axis_size("ctx")
-    stride4 = [[j + 4 * q for q in range(4)] for j in range(4)]
-
+    far = [[twin(4 * q + j) for q in range(4)] for j in range(4)]
+    v = twin(t)
+
+    chunks = queries.reshape(8, 2, 16, hd)
+    first_goes = (jnp.arange(8, dtype=jnp.int32) // 4 != v % 2)[:, None, None]
+    q_send = jnp.where(first_goes, chunks[:, 0], chunks[:, 1]).reshape(rows // 2, hd)
+    q_keep = jnp.where(first_goes, chunks[:, 1], chunks[:, 0]).reshape(rows // 2, hd)
+    q_send = jnp.concatenate([q_send[:, :half], q_send[:, half:]], axis=0)
     partner = swap(jnp.stack([key_heads, value_heads]), 0)
-    partner, gate_weight, up_weight = lax.optimization_barrier((partner, gate_weight, up_weight))
-    weights = lax.all_gather(
-        jnp.concatenate([gate_weight, up_weight], axis=1), "ctx", axis=0, tiled=True
-    )
+    weights = jnp.concatenate([gate_weight, up_weight], axis=1)
+    weights = lax.all_gather(weights, "ctx", axis=0, tiled=True)
+    core = c % 2
+    weight_half = lax.dynamic_slice_in_dim(out_weight, core * half, half, axis=0)
+    weight_half = swap(weight_half, 0)
+    q_came = swap(q_send, 0)
+
     own_first = t % 2 == 0
     pos = c * rows + jnp.arange(rows, dtype=jnp.int32)
     cosine, sine = rope_angles(pos, hd)
@@ -142,11 +160,13 @@
     came = [
         lax.ppermute(block, "ctx", [(i, i + 2 * s) for i in range(n_ctx - 2 * s)])
         for s in range(FAR, 0, -1)
-    ] + [block]
-    mine = jnp.concatenate(came, axis=0)
-    other = lax.ppermute(mine, "ctx", [(i, i ^ 1) for i in range(n_ctx)])
+    ]
+    mine = jnp.concatenate(came + [block], axis=0)
+    both_cores = [(i, i ^ 1) for i in range(n_ctx)]
+    other = lax.ppermute(mine, "ctx", both_cores)
+    weight_rest = lax.ppermute(weight_half, "ctx", both_cores)
+    partner_weight = jnp.concatenate([weight_half, weight_rest], axis=0)
     chip = c // 2
-    core = c % 2
     first_of = (chip - FAR + jnp.arange(FAR + 1, dtype=jnp.int32)) * 2
     inner = jnp.arange(rows, dtype=jnp.int32)
     pos_mine = ((first_of + core) * rows)[:, None] + inner[None, :]
@@ -155,23 +175,31 @@
     kv = jnp.concatenate([mine, other], axis=0)
     key_rows, value_rows = (kv[:, :hd], kv[:, hd:])
 
-    way = [1 - 2 * ((t + chain) % 2) for chain in range(2)]
-
-    def leave(a):
-        a = a.reshape(4, 4, 2, PIECE, *a.shape[1:])
-
-        def of(chain, r):
-            one = lax.dynamic_index_in_dim(a[:, :, chain], (t + r) % 4, 1, keepdims=False)
-            return one.reshape(4 * PIECE, *a.shape[4:])
-
-        return jnp.concatenate(
-            [of(x, r) for x in range(2) for r in (2, 4 + way[x])]
-            + [of(x, r) for x in range(2) for r in (4 - way[x], 0)],
-            axis=0,
-        )
-
-    q_rows = leave(rotate(queries[:, :half], queries[:, half:], cosine, sine))
-    q_pos = leave(pos)
+    upper = (v // 2) % 2 == 1
+
+    def by_class(a):
+        a = a.reshape(4, 2, 16, *a.shape[1:])
+        leave = jnp.where(upper, a[:, 0], a[:, 1])
+        stay = jnp.where(upper, a[:, 1], a[:, 0])
+        return jnp.concatenate([leave, stay], axis=0).reshape(rows // 2, *a.shape[3:])
+
+    w = 2 * jnp.arange(8, dtype=jnp.int32) + v % 2
+    share_pos = by_class(
+        (c * rows + twin(w)[:, None] * 16 + jnp.arange(16, dtype=jnp.int32)[None, :]).reshape(-1)
+    )
+    q_cos, q_sin = rope_angles(share_pos, hd)
+
+    def turned(lo, hi):
+        return rotate(by_class(lo), by_class(hi), q_cos, q_sin)
+
+    q_rows = jnp.concatenate(
+        [
+            turned(q_keep[:, :half], q_keep[:, half:]),
+            turned(q_came[: rows // 2], q_came[rows // 2 :]),
+        ],
+        axis=0,
+    )
+    q_pos = jnp.concatenate([share_pos, share_pos])
     q_doc = doc_of(q_pos, doc_blocks)
     key_doc = doc_of(jnp.maximum(key_pos, 0), doc_blocks)
     scores = lax.dot_general(
@@ -187,18 +215,21 @@
     numerator = jnp.dot(probs, value_rows, preferred_element_type=f32)
     denominator = jnp.sum(probs.astype(f32), axis=1)
     attended = (numerator / denominator[:, None]).astype(bf16)
+    beside = attended[rows // 2 :]
+    turned_round = jnp.concatenate([beside[:, half:], beside[:, :half]], axis=1)
+    both_heads = (attended[: rows // 2], jnp.where(core == 0, beside, turned_round))
 
     def out(a):
-        return jnp.dot(attended[a : a + 64], out_weight, preferred_element_type=f32).astype(bf16)
-
-    sent = [swap(out(64 * x), x) for x in range(2)]
-    kept = [out(128 + 64 * x) for x in range(2)]
-    both = [kept[x].astype(f32) + sent[x].astype(f32) for x in range(2)]
-    again = [swap(both[x][:32].astype(bf16), 1 - x) for x in range(2)]
-    sums = [(both[x][32:] + again[x].astype(f32)).astype(bf16) for x in range(2)]
-
-    sums = jnp.stack([a.reshape(4, PIECE, d) for a in sums], axis=1).reshape(4, 2 * PIECE, d)
-    parts = lax.all_to_all(sums, "tensor", 0, 0, tiled=True, axis_index_groups=stride4)
+        return jnp.dot(
+            both_heads[0][a : a + 64], out_weight, preferred_element_type=f32
+        ) + jnp.dot(both_heads[1][a : a + 64], partner_weight, preferred_element_type=f32)
+
+    leaves = out(0).astype(bf16)
+    sent = [swap_pairs(leaves[32 * x : 32 * (x + 1)], x) for x in range(2)]
+    sums = out(64) + jnp.concatenate(sent, axis=0).astype(f32)
+    parts = lax.all_to_all(
+        sums.astype(bf16).reshape(4, 16, d), "tensor", 0, 0, tiled=True, axis_index_groups=far
+    )
     attn_rows = jnp.sum(parts.astype(f32), axis=0)
     mixed = (residual.astype(f32) + rms_scale(attn_rows) * post_gain).astype(bf16)
     ffn_in = (rms_scale(mixed.astype(f32)) * ffn_gain).astype(bf16)

time: 197 us -> 194 us (0.985)
  the two profiles are of different devices: /device:TPU:24 before, /device:TPU:6 now
where the time goes in v1:
time: 194 us; the launch traced here: 191 us
  blocking collectives  69.7 us (36%)
  starting transfers between devices  45.6 us (24%)
  waiting for transfers between devices  27.8 us (14%)
  Pallas kernels  15.4 us (8%)
  between operations  14.8 us (8%)
  other arithmetic  10.1 us (5%)
  matrix products  3.79 us (2%)
  local copies, waits for them, and re-layouts  3.48 us (2%)
    all_to_all x1, blocking collectives, per_device(): lax.all_to_all(sums.astype(bf16).reshape(4, 16, d), 'tensor', 0, 0, tiled...  38.1 us
    all_gather x1, blocking collectives, per_device(): lax.all_gather(ffn_in, 'tensor', axis=0, tiled=True, axis_index_groups=st...  31.6 us
    ppermute x4, waiting for transfers between devices, per_device(): lax.ppermute(block, 'ctx', [(i, i + 2 * s) for i in range(n_ctx - 2 * s)])  18.2 us
    ppermute x5, starting transfers between devices, swap(): return lax.ppermute(value, 'tensor', ends + [(j, i) for i, j in ends])  17.7 us
    pallas_call x2, Pallas kernels, ffn(): pl.pallas_call(lambda *refs: ffn_kernel(steps, ff, len(pieces), *refs), o...  15.4 us
    ppermute x4, starting transfers between devices, per_device(): lax.ppermute(block, 'ctx', [(i, i + 2 * s) for i in range(n_ctx - 2 * s)])  12.9 us
    ppermute x2, starting transfers between devices, swap_pairs(): return lax.ppermute(value, 'tensor', ends + [(j, i) for i, j in ends])  10.6 us
    ppermute x2, waiting for transfers between devices, swap_pairs(): return lax.ppermute(value, 'tensor', ends + [(j, i) for i, j in ends])  7.44 us
  transfers between devices with their start and end apart: 14, of which 5 were waited for; matrix products, arithmetic and copies ran while one was open for 7% of the time, Pallas kernels for 4%

profile of v1, /device:TPU:6, one launch (start us, length us, event | category | flops | bytes accessed | tf_op | source)
XLA Modules:
  0.0 190.6 jit_solution(8598525813033030921)
XLA Ops:
  7.2 0.0 copy-start
  7.2 0.0 all-gather.2.cloned.1.call-start
  7.3 2.2 %pad_maximum_fusion = bf16[224,1792]{1,0:T(8,128)(2,1)} fusion(bf16[224,896]{1,0:T(8,128)(2,1)} %param.19, bf16[224,896]{1,0:T(8,128)(2,1)} %param.18), kind=kLoop, calls=%fused_computation.18 | loop fusion | flops 1605632 | bytes 1605632 | tf_op jit(solution)/shard_map/concatenate | solution.py:145
  9.5 0.0 all-gather.2.cloned.1.call-update
  9.5 0.1 broadcast_in_dim.18
  9.6 0.1 broadcast_in_dim.19
  9.7 0.1 bitcast_select_fusion.1
  9.8 0.6 pad_maximum_fusion.3
  10.5 3.8 %collective-permute-start = (bf16[256,128]{1,0:T(8,128)(2,1)}, bf16[256,128]{1,0:T(8,128)(2,1)}, u32[]{:S(2)}, u32[]{:S(2)}) collective-permute-start(bf16[256,128]{1,0:T(8,128)(2,1)} %pad_maximum_fusion.3), channel_id=1, source_target_pairs={{0,1},{2,3},{4,5},{6,7},{8,9},{10,11},{12,13},{14,15},{1,0},{3,2},... | collective-permute-start | bytes 196616 | tf_op jit(solution)/shard_map/ppermute | solution.py:22
  14.3 2.0 %collective-permute-start.1 = (bf16[2,256,128]{2,1,0:T(8,128)(2,1)S(1)}, bf16[2,256,128]{2,1,0:T(8,128)(2,1)S(1)}, u32[]{:S(2)}, u32[]{:S(2)}) collective-permute-start(bf16[2,256,128]{2,1,0:T(8,128)(2,1)S(1)} %pad_maximum_fusion.2), channel_id=1, source_target_pairs={{0,1},{2,3},{4,5},{6,7},{8,9},{10,11},{12,13},{14,15},{1,0},{3,2},... | collective-permute-start | bytes 393224 | tf_op jit(solution)/shard_map/ppermute | solution.py:22
  16.4 1.0 constant_dynamic-slice_fusion
  17.4 3.8 %collective-permute-start.7 = (bf16[128,3584]{1,0:T(8,128)(2,1)}, bf16[128,3584]{1,0:T(8,128)(2,1)S(1)}, u32[]{:S(2)}, u32[]{:S(2)}) collective-permute-start(bf16[128,3584]{1,0:T(8,128)(2,1)} %constant_dynamic-slice_fusion), channel_id=1, source_target_pairs={{0,1},{2,3},{4,5},{6,7},{8,9},{10,11},{12,13},{14,15},{1,0},{3,2},... | collective-permute-start | bytes 2752520 | tf_op jit(solution)/shard_map/ppermute | solution.py:22
  21.3 0.1 iota_add_fusion.2
  21.4 0.1 reshape.338
  21.5 0.2 reduce-window.8
  21.7 0.1 iota_add_fusion.1
  21.7 0.1 iota_add_fusion
  21.8 0.5 fusion.71
  22.4 0.6 select_bitcast_fusion.3
  23.0 0.6 pad_maximum_fusion.4
  23.6 0.7 convert_reduce_fusion.3
  24.3 0.6 broadcast_compare_fusion
  25.0 0.7 convert_reduce_fusion.2
  25.7 0.6 fusion.25
  26.3 5.1 %collective-permute-start.2 = (bf16[256,512]{1,0:T(8,128)(2,1)S(1)}, bf16[256,512]{1,0:T(8,128)(2,1)S(1)}, u32[]{:S(2)}, u32[]{:S(2)}) collective-permute-start(bf16[256,512]{1,0:T(8,128)(2,1)S(1)} %pad_maximum_fusion.1), channel_id=1, source_target_pairs={{0,128},{16,144},{32,160},{48,176},{64,192},{80,208},{96,224},{112... | collective-permute-start | bytes 786440 | tf_op jit(solution)/shard_map/ppermute | solution.py:161
  31.4 1.3 pad_maximum_fusion.5
  32.8 1.9 %collective-permute-start.3 = (bf16[256,512]{1,0:T(8,128)(2,1)S(1)}, bf16[256,512]{1,0:T(8,128)(2,1)S(1)}, u32[]{:S(2)}, u32[]{:S(2)}) collective-permute-start(bf16[256,512]{1,0:T(8,128)(2,1)S(1)} %pad_maximum_fusion.1), channel_id=1, source_target_pairs={{0,96},{16,112},{32,128},{48,144},{64,160},{80,176},{96,192},{112,... | collective-permute-start | bytes 786440 | tf_op jit(solution)/shard_map/ppermute | solution.py:161
  34.7 1.9 %collective-permute-start.4 = (bf16[256,512]{1,0:T(8,128)(2,1)S(1)}, bf16[256,512]{1,0:T(8,128)(2,1)S(1)}, u32[]{:S(2)}, u32[]{:S(2)}) collective-permute-start(bf16[256,512]{1,0:T(8,128)(2,1)S(1)} %pad_maximum_fusion.1), channel_id=1, source_target_pairs={{0,64},{16,80},{32,96},{48,112},{64,128},{80,144},{96,160},{112,17... | collective-permute-start | bytes 786440 | tf_op jit(solution)/shard_map/ppermute | solution.py:161
  36.6 0.8 fusion.69
  37.4 3.9 %collective-permute-start.5 = (bf16[256,512]{1,0:T(8,128)(2,1)S(1)}, bf16[256,512]{1,0:T(8,128)(2,1)S(1)}, u32[]{:S(2)}, u32[]{:S(2)}) collective-permute-start(bf16[256,512]{1,0:T(8,128)(2,1)S(1)} %pad_maximum_fusion.1), channel_id=1, source_target_pairs={{0,32},{16,48},{32,64},{48,80},{64,96},{80,112},{96,128},{112,144}... | collective-permute-start | bytes 786440 | tf_op jit(solution)/shard_map/ppermute | solution.py:161
  41.4 0.0 copy-start.6
  41.4 12.3 %collective-permute-done.3 = bf16[256,512]{1,0:T(8,128)(2,1)S(1)} collective-permute-done((bf16[256,512]{1,0:T(8,128)(2,1)S(1)}, bf16[256,512]{1,0:T(8,128)(2,1)S(1)}, u32[]{:S(2)}, u32[]{:S(2)}) %collective-permute-start.3) | collective-permute-done | bytes 262176 | tf_op jit(solution)/shard_map/ppermute | solution.py:161
  53.8 3.9 %collective-permute-done.4 = bf16[256,512]{1,0:T(8,128)(2,1)S(1)} collective-permute-done((bf16[256,512]{1,0:T(8,128)(2,1)S(1)}, bf16[256,512]{1,0:T(8,128)(2,1)S(1)}, u32[]{:S(2)}, u32[]{:S(2)}) %collective-permute-start.4) | collective-permute-done | bytes 262176 | tf_op jit(solution)/shard_map/ppermute | solution.py:161
  57.7 2.1 %collective-permute-done.5 = bf16[256,512]{1,0:T(8,128)(2,1)S(1)} collective-permute-done((bf16[256,512]{1,0:T(8,128)(2,1)S(1)}, bf16[256,512]{1,0:T(8,128)(2,1)S(1)}, u32[]{:S(2)}, u32[]{:S(2)}) %collective-permute-start.5) | collective-permute-done | bytes 262176 | tf_op jit(solution)/shard_map/ppermute | solution.py:161
  59.8 1.9 %collective-permute-start.6 = (bf16[1280,512]{1,0:T(8,128)(2,1)S(1)}, bf16[1280,512]{1,0:T(8,128)(2,1)S(1)}, u32[]{:S(2)}, u32[]{:S(2)}) collective-permute-start(bf16[1280,512]{1,0:T(8,128)(2,1)S(1)} %get-tuple-element.12), channel_id=1, source_target_pairs={{0,16},{16,0},{32,48},{48,32},{64,80},{80,64},{96,112},{112,96},{1... | collective-permute-start | bytes 3932168 | tf_op jit(solution)/shard_map/ppermute | solution.py:166
  61.9 0.4 fusion.44
  62.3 2.4 %collective-permute-start.8 = (bf16[128,3584]{1,0:T(8,128)(2,1)S(1)}, bf16[128,3584]{1,0:T(8,128)(2,1)S(1)}, u32[]{:S(2)}, u32[]{:S(2)}) collective-permute-start(bf16[128,3584]{1,0:T(8,128)(2,1)S(1)} %collective-permute-done.7), channel_id=1, source_target_pairs={{0,16},{16,0},{32,48},{48,32},{64,80},{80,64},{96,112},{112,96},{1... | collective-permute-start | bytes 2752520 | tf_op jit(solution)/shard_map/ppermute | solution.py:167
  64.7 0.1 constant_dynamic-update-slice_fusion.14
  64.8 0.1 constant_dynamic-update-slice_fusion.7
  64.9 1.5 convert_reduce_fusion
  66.4 0.5 fusion.14
  67.0 0.4 fusion.52
  67.4 0.1 constant_dynamic-update-slice_fusion.13
  67.5 0.5 fusion.2
  68.0 7.7 %collective-permute-start.10 = (bf16[32,3584]{1,0:T(8,128)(2,1)S(1)}, bf16[32,3584]{1,0:T(8,128)(2,1)S(1)}, u32[]{:S(2)}, u32[]{:S(2)}) collective-permute-start(bf16[32,3584]{1,0:T(8,128)(2,1)S(1)} %get-tuple-element.11), channel_id=1, source_target_pairs={{2,4},{3,5},{6,9},{7,8},{11,13},{10,12},{15,0},{14,1},{4,2},{5,3},... | collective-permute-start | bytes 688136 | tf_op jit(solution)/shard_map/ppermute | solution.py:28
  75.7 2.9 %collective-permute-start.9 = (bf16[32,3584]{1,0:T(8,128)(2,1)S(1)}, bf16[32,3584]{1,0:T(8,128)(2,1)S(1)}, u32[]{:S(2)}, u32[]{:S(2)}) collective-permute-start(bf16[32,3584]{1,0:T(8,128)(2,1)S(1)} %get-tuple-element.10), channel_id=1, source_target_pairs={{0,2},{1,3},{4,6},{5,7},{9,11},{8,10},{13,15},{12,14},{2,0},{3,1},... | collective-permute-start | bytes 688136 | tf_op jit(solution)/shard_map/ppermute | solution.py:28
  78.6 0.4 fusion.55
  79.1 7.4 %collective-permute-done.10 = bf16[32,3584]{1,0:T(8,128)(2,1)S(1)} collective-permute-done((bf16[32,3584]{1,0:T(8,128)(2,1)S(1)}, bf16[32,3584]{1,0:T(8,128)(2,1)S(1)}, u32[]{:S(2)}, u32[]{:S(2)}) %collective-permute-start.10) | collective-permute-done | bytes 229408 | tf_op jit(solution)/shard_map/ppermute | solution.py:28
  86.5 0.0 collective-permute-done.9
  86.5 0.5 fusion.1
  87.0 0.0 copy-start.12
  87.0 0.0 copy-start.11
  87.0 38.1 %all_to_all.5 = bf16[4,16,3584]{2,1,0:T(8,128)(2,1)S(1)} all-to-all(bf16[4,16,3584]{2,1,0:T(8,128)(2,1)S(1)} %bitcast.127), channel_id=1, replica_groups={{0,4,9,13},{1,5,8,12},{2,6,11,15},{3,7,10,14},{16,20,25,29},{17,21,24,2..., dimensions={0} | all-to-all | bytes 917504 | tf_op jit(solution)/shard_map/all_to_all | solution.py:230
  125.1 0.1 convert_reduce_fusion.1
  125.2 0.1 multiply_reduce_fusion
  125.3 0.2 fusion.17
  125.6 0.1 fusion.19
  125.7 31.6 %all_gather.6.refs_1_ = bf16[128,3584]{1,0:T(8,128)(2,1)S(1)} all-gather(bf16[16,3584]{1,0:T(8,128)(2,1)S(1)} %fusion.19), channel_id=1, replica_groups={{0,2,4,6,8,10,12,14},{1,3,5,7,9,11,13,15},{16,18,20,22,24,26,28,30},{17..., dimensions={0}, use_global_device_ids=true | all-gather | bytes 1032192 | tf_op jit(solution)/shard_map/all_gather | solution.py:238
  157.2 0.9 fusion.64
  158.2 6.1 %collective-permute-start.11 = (bf16[64,3584]{1,0:T(8,128)(2,1)}, bf16[64,3584]{1,0:T(8,128)(2,1)}, u32[]{:S(2)}, u32[]{:S(2)}) collective-permute-start(bf16[64,3584]{1,0:T(8,128)(2,1)} %get-tuple-element.9), channel_id=1, source_target_pairs={{0,1},{2,3},{4,5},{6,7},{8,9},{10,11},{12,13},{14,15},{1,0},{3,2},... | collective-permute-start | bytes 1376264 | tf_op jit(solution)/shard_map/ppermute | solution.py:22
  164.3 1.9 %collective-permute-start.12 = (bf16[64,3584]{1,0:T(8,128)(2,1)S(1)}, bf16[64,3584]{1,0:T(8,128)(2,1)}, u32[]{:S(2)}, u32[]{:S(2)}) collective-permute-start(bf16[64,3584]{1,0:T(8,128)(2,1)S(1)} %get-tuple-element.8), channel_id=1, source_target_pairs={{1,2},{3,4},{5,6},{7,8},{9,10},{11,12},{13,14},{15,0},{2,1},{4,3},... | collective-permute-start | bytes 1376264 | tf_op jit(solution)/shard_map/ppermute | solution.py:22
  166.2 7.6 %ffn.2.refs_4_ = bf16[128,896]{1,0:T(8,128)(2,1)} custom-call(s32[1]{0:T(128)} %bitcast.35.refs_0_, bf16[128,3584]{1,0:T(8,128)(2,1)} %copy-done.1, bf16[3584,1792]{1,0:T(8,128)(2,1)} %all-gather.2.cloned.1.call-done.refs_2_.refs_3_), custom_call_target="tpu_custom_call" | custom-call | flops 1644167168 | bytes 12845056 | tf_op jit(solution)/shard_map/ffn/pallas_call | solution.py:95
  173.9 2.1 %collective-permute-done.12.refs_2_ = bf16[64,3584]{1,0:T(8,128)(2,1)} collective-permute-done((bf16[64,3584]{1,0:T(8,128)(2,1)S(1)}, bf16[64,3584]{1,0:T(8,128)(2,1)}, u32[]{:S(2)}, u32[]{:S(2)}) %collective-permute-start.12) | collective-permute-done | bytes 458784 | tf_op jit(solution)/shard_map/ppermute | solution.py:22
  176.0 7.8 %ffn.3 = bf16[8,2,16,896]{3,2,1,0:T(8,128)(2,1)} custom-call(s32[1]{0:T(128)} %bitcast.35.refs_0_, bf16[64,3584]{1,0:T(8,128)(2,1)} %collective-permute-done.11.refs_1_, bf16[64,3584]{1,0:T(8,128)(2,1)} %collective-permute-done.12.refs_2_, bf16[3584,1792]{1,0:T(8,128)(2,1)} %all-gather.2.cloned.1.call-done.refs_2_.refs_3_, bf16[128,896]{1,0:T(8,128)(2,1)} %ffn.2.refs_4_), custom_call_target="tpu_custom_call" | custom-call | flops 1644167168 | bytes 12845056 | tf_op jit(solution)/shard_map/ffn/pallas_call | solution.py:95
  (84 shorter events, 0.6 us)
Async XLA Ops:
  7.2 9.2 %copy-start = (bf16[256,3584]{1,0:T(8,128)(2,1)S(1)}, bf16[256,3584]{1,0:T(8,128)(2,1)}, u32[]{:S(2)}) copy-start(bf16[256,3584]{1,0:T(8,128)(2,1)} %param.15) | copy-start | bytes 5505028
  7.2 2.5 %copy-start.5 = (bf16[256,256]{1,0:T(8,128)(2,1)S(1)}, bf16[256,256]{1,0:T(8,128)(2,1)}, u32[]{:S(2)}) copy-start(bf16[256,256]{1,0:T(8,128)(2,1)} %param.11) | copy-start | bytes 393220
  7.2 7.1 %copy-start.4 = (bf16[256,128]{1,0:T(8,128)(2,1)S(1)}, bf16[256,128]{1,0:T(8,128)(2,1)}, u32[]{:S(2)}) copy-start(bf16[256,128]{1,0:T(8,128)(2,1)} %param.12) | copy-start | bytes 196612
  7.2 7.1 %copy-start.3 = (bf16[256,128]{1,0:T(8,128)(2,1)S(1)}, bf16[256,128]{1,0:T(8,128)(2,1)}, u32[]{:S(2)}) copy-start(bf16[256,128]{1,0:T(8,128)(2,1)} %param.13) | copy-start | bytes 196612
  7.2 150.0 %all-gather.2.cloned.1.call-start = ((), (), s32[]{:S(2)}) async-start(), calls=%async_computation.1 | async-start | bytes 13647872 | tf_op jit(solution)/shard_map/all_gather | solution.py:146
  9.5 12.0 %copy-start.21 = (s32[6]{0:T(128)S(1)}, s32[6]{0:T(128)}, u32[]{:S(2)}) copy-start(s32[6]{0:T(128)} %param.14) | copy-start | bytes 76
  10.5 26.1 %collective-permute-start = (bf16[256,128]{1,0:T(8,128)(2,1)}, bf16[256,128]{1,0:T(8,128)(2,1)}, u32[]{:S(2)}, u32[]{:S(2)}) collective-permute-start(bf16[256,128]{1,0:T(8,128)(2,1)} %pad_maximum_fusion.3), channel_id=1, source_target_pairs={{0,1},{2,3},{4,5},{6,7},{8,9},{10,11},{12,13},{14,15},{1,0},{3,2},... | collective-permute-start | bytes 196616 | tf_op jit(solution)/shard_map/ppermute | solution.py:22
  14.3 11.3 %collective-permute-start.1 = (bf16[2,256,128]{2,1,0:T(8,128)(2,1)S(1)}, bf16[2,256,128]{2,1,0:T(8,128)(2,1)S(1)}, u32[]{:S(2)}, u32[]{:S(2)}) collective-permute-start(bf16[2,256,128]{2,1,0:T(8,128)(2,1)S(1)} %pad_maximum_fusion.2), channel_id=1, source_target_pairs={{0,1},{2,3},{4,5},{6,7},{8,9},{10,11},{12,13},{14,15},{1,0},{3,2},... | collective-permute-start | bytes 393224 | tf_op jit(solution)/shard_map/ppermute | solution.py:22
  17.4 44.9 %collective-permute-start.7 = (bf16[128,3584]{1,0:T(8,128)(2,1)}, bf16[128,3584]{1,0:T(8,128)(2,1)S(1)}, u32[]{:S(2)}, u32[]{:S(2)}) collective-permute-start(bf16[128,3584]{1,0:T(8,128)(2,1)} %constant_dynamic-slice_fusion), channel_id=1, source_target_pairs={{0,1},{2,3},{4,5},{6,7},{8,9},{10,11},{12,13},{14,15},{1,0},{3,2},... | collective-permute-start | bytes 2752520 | tf_op jit(solution)/shard_map/ppermute | solution.py:22
  22.4 2.6 %copy-start.18 = (s32[256]{0:T(256)}, s32[256]{0:T(256)S(1)}, u32[]{:S(2)}) copy-start(s32[256]{0:T(256)S(1)} %constant_dynamic-update-slice_fusion.16) | copy-start | bytes 3076
  22.4 3.3 %copy-start.9 = (s32[2560]{0:T(1024)}, s32[2560]{0:T(1024)S(1)}, u32[]{:S(2)}) copy-start(s32[2560]{0:T(1024)S(1)} %constant_dynamic-update-slice_fusion.15) | copy-start | bytes 30724
  24.9 1.3 copy-start.15
  26.3 15.0 %collective-permute-start.2 = (bf16[256,512]{1,0:T(8,128)(2,1)S(1)}, bf16[256,512]{1,0:T(8,128)(2,1)S(1)}, u32[]{:S(2)}, u32[]{:S(2)}) collective-permute-start(bf16[256,512]{1,0:T(8,128)(2,1)S(1)} %pad_maximum_fusion.1), channel_id=1, source_target_pairs={{0,128},{16,144},{32,160},{48,176},{64,192},{80,208},{96,224},{112... | collective-permute-start | bytes 786440 | tf_op jit(solution)/shard_map/ppermute | solution.py:161
  32.8 21.0 %collective-permute-start.3 = (bf16[256,512]{1,0:T(8,128)(2,1)S(1)}, bf16[256,512]{1,0:T(8,128)(2,1)S(1)}, u32[]{:S(2)}, u32[]{:S(2)}) collective-permute-start(bf16[256,512]{1,0:T(8,128)(2,1)S(1)} %pad_maximum_fusion.1), channel_id=1, source_target_pairs={{0,96},{16,112},{32,128},{48,144},{64,160},{80,176},{96,192},{112,... | collective-permute-start | bytes 786440 | tf_op jit(solution)/shard_map/ppermute | solution.py:161
  34.7 23.0 %collective-permute-start.4 = (bf16[256,512]{1,0:T(8,128)(2,1)S(1)}, bf16[256,512]{1,0:T(8,128)(2,1)S(1)}, u32[]{:S(2)}, u32[]{:S(2)}) collective-permute-start(bf16[256,512]{1,0:T(8,128)(2,1)S(1)} %pad_maximum_fusion.1), channel_id=1, source_target_pairs={{0,64},{16,80},{32,96},{48,112},{64,128},{80,144},{96,160},{112,17... | collective-permute-start | bytes 786440 | tf_op jit(solution)/shard_map/ppermute | solution.py:161
  37.4 22.4 %collective-permute-start.5 = (bf16[256,512]{1,0:T(8,128)(2,1)S(1)}, bf16[256,512]{1,0:T(8,128)(2,1)S(1)}, u32[]{:S(2)}, u32[]{:S(2)}) collective-permute-start(bf16[256,512]{1,0:T(8,128)(2,1)S(1)} %pad_maximum_fusion.1), channel_id=1, source_target_pairs={{0,32},{16,48},{32,64},{48,80},{64,96},{80,112},{96,128},{112,144}... | collective-permute-start | bytes 786440 | tf_op jit(solution)/shard_map/ppermute | solution.py:161
  41.4 20.4 %copy-start.6 = (bf16[8,16,128]{2,1,0:T(8,128)(2,1)S(1)}, bf16[8,16,128]{2,1,0:T(8,128)(2,1)}, u32[]{:S(2)}) copy-start(bf16[8,16,128]{2,1,0:T(8,128)(2,1)} %pad_maximum_fusion.4) | copy-start | bytes 98308
  41.4 20.4 %copy-start.7 = (bf16[8,16,128]{2,1,0:T(8,128)(2,1)S(1)}, bf16[8,16,128]{2,1,0:T(8,128)(2,1)}, u32[]{:S(2)}) copy-start(bf16[8,16,128]{2,1,0:T(8,128)(2,1)} %pad_maximum_fusion.5) | copy-start | bytes 98308
  41.4 20.4 %copy-start.16 = (f32[128]{0:T(128)S(1)}, f32[128]{0:T(128)}, u32[]{:S(2)}) copy-start(f32[128]{0:T(128)} %copy-done.15) | copy-start | bytes 1540
  41.4 20.4 %copy-start.20 = (f32[128]{0:T(128)S(1)}, f32[128]{0:T(128)}, u32[]{:S(2)}) copy-start(f32[128]{0:T(128)} %get-tuple-element.52) | copy-start | bytes 1540
  59.8 4.9 %collective-permute-start.6 = (bf16[1280,512]{1,0:T(8,128)(2,1)S(1)}, bf16[1280,512]{1,0:T(8,128)(2,1)S(1)}, u32[]{:S(2)}, u32[]{:S(2)}) collective-permute-start(bf16[1280,512]{1,0:T(8,128)(2,1)S(1)} %get-tuple-element.12), channel_id=1, source_target_pairs={{0,16},{16,0},{32,48},{48,32},{64,80},{80,64},{96,112},{112,96},{1... | collective-permute-start | bytes 3932168 | tf_op jit(solution)/shard_map/ppermute | solution.py:166
  62.2 2.7 %copy-start.10 = (s32[2560]{0:T(1024)S(1)}, s32[2560]{0:T(1024)}, u32[]{:S(2)}) copy-start(s32[2560]{0:T(1024)} %copy-done.9) | copy-start | bytes 30724
  62.2 2.7 %copy-start.13 = (s32[2560]{0:T(1024)S(1)}, s32[2560]{0:T(1024)}, u32[]{:S(2)}) copy-start(s32[2560]{0:T(1024)} %convert_reduce_fusion.2) | copy-start | bytes 30724
  62.3 2.7 %copy-start.14 = (pred[2560]{0:T(1024)(128)(4,1)S(1)}, pred[2560]{0:T(1024)(128)(4,1)}, u32[]{:S(2)}) copy-start(pred[2560]{0:T(1024)(128)(4,1)} %broadcast_compare_fusion) | copy-start | bytes 7684
  62.3 2.7 %copy-start.17 = (s32[256]{0:T(256)S(1)}, s32[256]{0:T(256)}, u32[]{:S(2)}) copy-start(s32[256]{0:T(256)} %convert_reduce_fusion.3) | copy-start | bytes 3076
  62.3 2.7 %copy-start.19 = (s32[256]{0:T(256)S(1)}, s32[256]{0:T(256)}, u32[]{:S(2)}) copy-start(s32[256]{0:T(256)} %copy-done.18) | copy-start | bytes 3076
  62.3 5.1 %collective-permute-start.8 = (bf16[128,3584]{1,0:T(8,128)(2,1)S(1)}, bf16[128,3584]{1,0:T(8,128)(2,1)S(1)}, u32[]{:S(2)}, u32[]{:S(2)}) collective-permute-start(bf16[128,3584]{1,0:T(8,128)(2,1)S(1)} %collective-permute-done.7), channel_id=1, source_target_pairs={{0,16},{16,0},{32,48},{48,32},{64,80},{80,64},{96,112},{112,96},{1... | collective-permute-start | bytes 2752520 | tf_op jit(solution)/shard_map/ppermute | solution.py:167
  68.0 18.5 %collective-permute-start.10 = (bf16[32,3584]{1,0:T(8,128)(2,1)S(1)}, bf16[32,3584]{1,0:T(8,128)(2,1)S(1)}, u32[]{:S(2)}, u32[]{:S(2)}) collective-permute-start(bf16[32,3584]{1,0:T(8,128)(2,1)S(1)} %get-tuple-element.11), channel_id=1, source_target_pairs={{2,4},{3,5},{6,9},{7,8},{11,13},{10,12},{15,0},{14,1},{4,2},{5,3},... | collective-permute-start | bytes 688136 | tf_op jit(solution)/shard_map/ppermute | solution.py:28
  75.7 10.8 %collective-permute-start.9 = (bf16[32,3584]{1,0:T(8,128)(2,1)S(1)}, bf16[32,3584]{1,0:T(8,128)(2,1)S(1)}, u32[]{:S(2)}, u32[]{:S(2)}) collective-permute-start(bf16[32,3584]{1,0:T(8,128)(2,1)S(1)} %get-tuple-element.10), channel_id=1, source_target_pairs={{0,2},{1,3},{4,6},{5,7},{9,11},{8,10},{13,15},{12,14},{2,0},{3,1},... | collective-permute-start | bytes 688136 | tf_op jit(solution)/shard_map/ppermute | solution.py:28
  87.0 38.3 %copy-start.8 = (bf16[16,3584]{1,0:T(8,128)(2,1)S(1)}, bf16[16,3584]{1,0:T(8,128)(2,1)}, u32[]{:S(2)}) copy-start(bf16[16,3584]{1,0:T(8,128)(2,1)} %param.10) | copy-start | bytes 344068
  87.0 38.3 %copy-start.12 = (f32[3584]{0:T(1024)S(1)}, f32[3584]{0:T(1024)}, u32[]{:S(2)}) copy-start(f32[3584]{0:T(1024)} %param.16) | copy-start | bytes 43012
  87.0 38.6 %copy-start.11 = (f32[3584]{0:T(1024)S(1)}, f32[3584]{0:T(1024)}, u32[]{:S(2)}) copy-start(f32[3584]{0:T(1024)} %param.17) | copy-start | bytes 43012
  125.6 48.3 %copy-start.2 = (bf16[16,3584]{1,0:T(8,128)(2,1)}, bf16[16,3584]{1,0:T(8,128)(2,1)S(1)}, u32[]{:S(2)}) copy-start(bf16[16,3584]{1,0:T(8,128)(2,1)S(1)} %get-tuple-element.7) | copy-start | bytes 344068
  157.2 9.0 %copy-start.1 = (bf16[128,3584]{1,0:T(8,128)(2,1)}, bf16[128,3584]{1,0:T(8,128)(2,1)S(1)}, u32[]{:S(2)}) copy-start(bf16[128,3584]{1,0:T(8,128)(2,1)S(1)} %all_gather.6.refs_1_) | copy-start | bytes 2752516
  158.2 15.7 %collective-permute-start.11 = (bf16[64,3584]{1,0:T(8,128)(2,1)}, bf16[64,3584]{1,0:T(8,128)(2,1)}, u32[]{:S(2)}, u32[]{:S(2)}) collective-permute-start(bf16[64,3584]{1,0:T(8,128)(2,1)} %get-tuple-element.9), channel_id=1, source_target_pairs={{0,1},{2,3},{4,5},{6,7},{8,9},{10,11},{12,13},{14,15},{1,0},{3,2},... | collective-permute-start | bytes 1376264 | tf_op jit(solution)/shard_map/ppermute | solution.py:22
  164.3 11.7 %collective-permute-start.12 = (bf16[64,3584]{1,0:T(8,128)(2,1)S(1)}, bf16[64,3584]{1,0:T(8,128)(2,1)}, u32[]{:S(2)}, u32[]{:S(2)}) collective-permute-start(bf16[64,3584]{1,0:T(8,128)(2,1)S(1)} %get-tuple-element.8), channel_id=1, source_target_pairs={{1,2},{3,4},{5,6},{7,8},{9,10},{11,12},{13,14},{15,0},{2,1},{4,3},... | collective-permute-start | bytes 1376264 | tf_op jit(solution)/shard_map/ppermute | solution.py:22
Sparse Core Ops, SparseCore 0:
  11.3 128.4 all-gather.1
